TPU v7x, 32 devices: a whole 2x2x4 slice. The times are simulated.
32 devices in a mesh: row: 8 (over z, core), col: 4 (over y, x).
Axes of the slice: x: 2, y: 2, z: 4, core: 2. Of those that a mesh axis runs over, the one named last changes fastest.
Arguments:
- attn_out: bfloat16 [6, 512, 2048], P(None, 'col', 'row'), may hold values from -0.625 to 0.625
- out_cotangent: bfloat16 [6, 512, 2048], P(None, 'row', 'col'), may hold values from -6 to 6
- frozen: bfloat16 [6, 2048, 2048], P(None, 'row', 'col'), may hold values from -0.5 to 0.5
- adapt_in: bfloat16 [6, 32, 2048], P(None, None, 'row'), may hold values from -0.125 to 0.125
- adapt_out: bfloat16 [6, 32, 2048], P(None, None, 'col'), may hold values from -1 to 1
- magnitude: float32 [6, 2048], P(None, 'col'), may hold values from 0.1 to 1.9
Outputs:
- input_grad: bfloat16 [6, 512, 2048], P(None, 'col', 'row')
- adapt_in_grad: float32 [6, 32, 2048], P(None, None, 'row')
- adapt_out_grad: float32 [6, 32, 2048], P(None, None, 'col')
- magnitude_grad: float32 [6, 2048], P(None, 'col')
All inputs are finite; a program needn't handle non-finite values.
Results may differ from a plain program's by a relative error of at most 0.0065.
Values may be sent and summed in bfloat16 or wider, within the bound.
A program may use at most 64 MiB of HBM per device.

v0:
```python
import jax
import jax.numpy as jnp
from jax import lax
from jax.sharding import PartitionSpec as P

precise = lax.Precision.HIGHEST


def one_layer(acts, grads, frozen, adapt_in, adapt_out, magnitude):
    merged = frozen.astype(jnp.float32) + lax.dot_general(
        adapt_in, adapt_out, (((0,), (0,)), ((), ())), preferred_element_type=jnp.float32
    )
    squares_part = jnp.sum(merged * merged, axis=0)
    grads_all = lax.all_gather(grads, "row", axis=0, tiled=True)
    outer = lax.dot_general(
        lax.all_gather(acts, "col", axis=0, tiled=True),
        grads_all,
        (((0,), (0,)), ((), ())),
        preferred_element_type=jnp.float32,
    )
    dots_part = jnp.sum(merged * outer, axis=0)
    adapt_in_wide = adapt_in.astype(jnp.float32)
    inner_outer = jnp.dot(adapt_in_wide, outer, precision=precise)
    inner_merged = jnp.dot(adapt_in_wide, merged, precision=precise)
    squares, dots, inner_outer, inner_merged = lax.psum(
        (squares_part, dots_part, inner_outer, inner_merged), "row"
    )
    norms = jnp.sqrt(squares + 0.25)
    scales = magnitude / norms
    correct = -magnitude * dots / (norms * norms * norms)
    delta = outer * scales + merged * correct
    out_grad = inner_outer * scales + inner_merged * correct
    magnitude_grad = dots / norms
    in_part = lax.dot_general(
        adapt_out.astype(jnp.float32), delta, (((1,), (1,)), ((), ())), precision=precise
    )
    in_grad = lax.psum(in_part, "col")
    scaled = (grads_all * scales).astype(jnp.bfloat16)
    weight_low = merged.astype(jnp.bfloat16)
    summed = lax.psum_scatter(
        lax.dot_general(
            scaled, weight_low, (((1,), (1,)), ((), ())), preferred_element_type=jnp.float32
        ),
        "col",
        scatter_dimension=0,
        tiled=True,
    )
    return (summed.astype(jnp.bfloat16), in_grad, out_grad, magnitude_grad)


def body(attn_out, out_cotangent, frozen, adapt_in, adapt_out, magnitude):
    results = [
        one_layer(
            attn_out[layer_at],
            out_cotangent[layer_at],
            frozen[layer_at],
            adapt_in[layer_at],
            adapt_out[layer_at],
            magnitude[layer_at],
        )
        for layer_at in range(frozen.shape[0])
    ]
    return (
        jnp.stack([item[0] for item in results]),
        jnp.stack([item[1] for item in results]),
        jnp.stack([item[2] for item in results]),
        jnp.stack([item[3] for item in results]),
    )


def solution(mesh):
    return jax.shard_map(
        body,
        mesh=mesh,
        in_specs=(
            P(None, "col", "row"),
            P(None, "row", "col"),
            P(None, "row", "col"),
            P(None, None, "row"),
            P(None, None, "col"),
            P(None, "col"),
        ),
        out_specs=(
            P(None, "col", "row"),
            P(None, None, "row"),
            P(None, None, "col"),
            P(None, "col"),
        ),
        check_vma=False,
    )
```

profile of v0, /device:TPU:0, one launch (start us, length us, event | category | flops | bytes accessed | tf_op | source)
XLA Modules:
  0.0 473.6 jit_solution(1073232057520900545)
XLA Ops:
  7.2 1.1 fusion.151
  8.3 16.5 %all-gather = bf16[1,512,512]{2,1,0:T(8,128)(2,1)S(1)} all-gather(bf16[1,64,512]{2,1,0:T(8,128)(2,1)S(1)} %get-tuple-element.56), channel_id=2, replica_groups=mesh['row'=8,'col'=4] {'row'}, dimensions={1}, use_global_device_ids=true | all-gather | bytes 589824 | tf_op jit(solution)/shard_map/all_gather | solution.py:14
  24.8 9.0 %all-gather.6 = bf16[1,512,256]{2,1,0:T(8,128)(2,1)S(1)} all-gather(bf16[1,128,256]{2,1,0:T(8,128)(2,1)S(1)} %get-tuple-element.50), channel_id=8, replica_groups=mesh['row'=8,'col'=4] {'col'}, dimensions={1}, use_global_device_ids=true | all-gather | bytes 327680 | tf_op jit(solution)/shard_map/all_gather | solution.py:16
  33.8 15.0 %all-gather.1 = bf16[1,512,512]{2,1,0:T(8,128)(2,1)S(1)} all-gather(bf16[1,64,512]{2,1,0:T(8,128)(2,1)S(1)} %get-tuple-element.55), channel_id=3, replica_groups=mesh['row'=8,'col'=4] {'row'}, dimensions={1}, use_global_device_ids=true | all-gather | bytes 589824 | tf_op jit(solution)/shard_map/all_gather | solution.py:14
  48.8 9.1 %all-gather.7 = bf16[1,512,256]{2,1,0:T(8,128)(2,1)S(1)} all-gather(bf16[1,128,256]{2,1,0:T(8,128)(2,1)S(1)} %get-tuple-element.49), channel_id=9, replica_groups=mesh['row'=8,'col'=4] {'col'}, dimensions={1}, use_global_device_ids=true | all-gather | bytes 327680 | tf_op jit(solution)/shard_map/all_gather | solution.py:16
  59.2 14.9 %all-gather.2 = bf16[1,512,512]{2,1,0:T(8,128)(2,1)S(1)} all-gather(bf16[1,64,512]{2,1,0:T(8,128)(2,1)S(1)} %get-tuple-element.54), channel_id=4, replica_groups=mesh['row'=8,'col'=4] {'row'}, dimensions={1}, use_global_device_ids=true | all-gather | bytes 589824 | tf_op jit(solution)/shard_map/all_gather | solution.py:14
  74.1 8.0 %all-gather.8 = bf16[1,512,256]{2,1,0:T(8,128)(2,1)S(1)} all-gather(bf16[1,128,256]{2,1,0:T(8,128)(2,1)S(1)} %get-tuple-element.48), channel_id=10, replica_groups=mesh['row'=8,'col'=4] {'col'}, dimensions={1}, use_global_device_ids=true | all-gather | bytes 327680 | tf_op jit(solution)/shard_map/all_gather | solution.py:16
  82.7 15.0 %all-gather.3 = bf16[1,512,512]{2,1,0:T(8,128)(2,1)S(1)} all-gather(bf16[1,64,512]{2,1,0:T(8,128)(2,1)S(1)} %get-tuple-element.53), channel_id=5, replica_groups=mesh['row'=8,'col'=4] {'row'}, dimensions={1}, use_global_device_ids=true | all-gather | bytes 589824 | tf_op jit(solution)/shard_map/all_gather | solution.py:14
  97.7 8.9 %all-gather.9 = bf16[1,512,256]{2,1,0:T(8,128)(2,1)S(1)} all-gather(bf16[1,128,256]{2,1,0:T(8,128)(2,1)S(1)} %get-tuple-element.47), channel_id=11, replica_groups=mesh['row'=8,'col'=4] {'col'}, dimensions={1}, use_global_device_ids=true | all-gather | bytes 327680 | tf_op jit(solution)/shard_map/all_gather | solution.py:16
  107.3 14.8 %all-gather.4 = bf16[1,512,512]{2,1,0:T(8,128)(2,1)S(1)} all-gather(bf16[1,64,512]{2,1,0:T(8,128)(2,1)S(1)} %get-tuple-element.57), channel_id=6, replica_groups=mesh['row'=8,'col'=4] {'row'}, dimensions={1}, use_global_device_ids=true | all-gather | bytes 589824 | tf_op jit(solution)/shard_map/all_gather | solution.py:14
  122.1 8.1 %all-gather.10 = bf16[1,512,256]{2,1,0:T(8,128)(2,1)S(1)} all-gather(bf16[1,128,256]{2,1,0:T(8,128)(2,1)S(1)} %get-tuple-element.51), channel_id=12, replica_groups=mesh['row'=8,'col'=4] {'col'}, dimensions={1}, use_global_device_ids=true | all-gather | bytes 327680 | tf_op jit(solution)/shard_map/all_gather | solution.py:16
  130.8 15.0 %all-gather.5 = bf16[1,512,512]{2,1,0:T(8,128)(2,1)S(1)} all-gather(bf16[1,64,512]{2,1,0:T(8,128)(2,1)S(1)} %get-tuple-element.52), channel_id=7, replica_groups=mesh['row'=8,'col'=4] {'row'}, dimensions={1}, use_global_device_ids=true | all-gather | bytes 589824 | tf_op jit(solution)/shard_map/all_gather | solution.py:14
  145.8 9.1 %all-gather.11 = bf16[1,512,256]{2,1,0:T(8,128)(2,1)S(1)} all-gather(bf16[1,128,256]{2,1,0:T(8,128)(2,1)S(1)} %get-tuple-element.46), channel_id=13, replica_groups=mesh['row'=8,'col'=4] {'col'}, dimensions={1}, use_global_device_ids=true | all-gather | bytes 327680 | tf_op jit(solution)/shard_map/all_gather | solution.py:16
  156.4 27.6 %all-reduce = (f32[512]{0:T(512)}, f32[512]{0:T(512)}, f32[512]{0:T(512)S(1)}, f32[512]{0:T(512)S(1)}, f32[512]{0:T(512)S(1)}, /*index=5*/f32[512]{0:T(512)S(1)}...) all-reduce(f32[512]{0:T(512)S(1)} %get-tuple-element.15, ...), channel_id=1, replica_groups=mesh['row'=8,'col'=4] {'row'}, use_global_device_ids=true, to_apply=%region_1.0 | all-reduce | flops 6144 | bytes 49152 | tf_op jit(solution)/shard_map/psum | solution.py:25
  184.9 2.1 convolution_bitcast_fusion.17
  187.0 2.1 convolution_bitcast_fusion.16
  189.2 1.0 convolution_bitcast_fusion.15
  194.6 2.0 convolution_bitcast_fusion.11
  205.9 2.2 fusion
  208.2 2.2 fusion.1
  210.5 1.2 fusion.2
  211.8 1.1 fusion.3
  213.0 1.1 fusion.4
  214.2 1.1 fusion.5
  216.0 18.9 %all-reduce.8.cloned.1.call-done = (f32[1,32,256]{2,1,0:T(8,128)}, f32[1,32,256]{2,1,0:T(8,128)}, f32[1,32,256]{2,1,0:T(8,128)}, f32[1,32,256]{2,1,0:T(8,128)}, ...) async-done(((f32[1,32,256]{2,1,0:T(8,128)}, f32[1,32,256]{2,1,0:T(8,128)}, f32[1,32,256]{2,1,0:T(8,128)}, f32[1,32,256]{2,1,0:T(8,128)}, f32[1,32,256]{2,1,0:T(8,128)}, ...) | async-done | bytes 196624 | tf_op jit(solution)/shard_map/psum | solution.py:37
  239.5 59.2 %all-reduce.6.cloned.1.call-done = (f32[32,512]{1,0:T(8,128)}, f32[32,512]{1,0:T(8,128)}, f32[32,512]{1,0:T(8,128)}, f32[32,512]{1,0:T(8,128)}, f32[32,512]{1,0:...) async-done(((f32[32,512]{1,0:T(8,128)}, f32[32,512]{1,0:T(8,128)}, ...) | async-done | bytes 786448 | tf_op jit(solution)/shard_map/psum | solution.py:25
  304.1 21.6 %reduce-scatter.7.cloned.1.call-done = f32[128,256]{1,0:T(8,128)} async-done(((f32[512,256]{1,0:T(8,128)}), f32[128,256]{1,0:T(8,128)}) %reduce-scatter.7.cloned.1.call-update) | async-done | bytes 131088 | tf_op jit(solution)/shard_map/reduce_scatter | solution.py:40
  326.6 26.9 %reduce-scatter.9.cloned.1.call-done = f32[128,256]{1,0:T(8,128)} async-done(((f32[512,256]{1,0:T(8,128)}), f32[128,256]{1,0:T(8,128)}) %reduce-scatter.9.cloned.1.call-update) | async-done | bytes 131088 | tf_op jit(solution)/shard_map/reduce_scatter | solution.py:40
  354.5 26.9 %reduce-scatter.11.cloned.1.call-done = f32[128,256]{1,0:T(8,128)} async-done(((f32[512,256]{1,0:T(8,128)}), f32[128,256]{1,0:T(8,128)}) %reduce-scatter.11.cloned.1.call-update) | async-done | bytes 131088 | tf_op jit(solution)/shard_map/reduce_scatter | solution.py:40
  382.3 26.9 %reduce-scatter.13.cloned.1.call-done = f32[128,256]{1,0:T(8,128)} async-done(((f32[512,256]{1,0:T(8,128)}), f32[128,256]{1,0:T(8,128)}) %reduce-scatter.13.cloned.1.call-update) | async-done | bytes 131088 | tf_op jit(solution)/shard_map/reduce_scatter | solution.py:40
  410.1 27.0 %reduce-scatter.15.cloned.1.call-done = f32[128,256]{1,0:T(8,128)} async-done(((f32[512,256]{1,0:T(8,128)}), f32[128,256]{1,0:T(8,128)}) %reduce-scatter.15.cloned.1.call-update) | async-done | bytes 131088 | tf_op jit(solution)/shard_map/reduce_scatter | solution.py:40
  438.0 27.0 %reduce-scatter.17.cloned.1.call-done = f32[128,256]{1,0:T(8,128)} async-done(((f32[512,256]{1,0:T(8,128)}), f32[128,256]{1,0:T(8,128)}) %reduce-scatter.17.cloned.1.call-update) | async-done | bytes 131088 | tf_op jit(solution)/shard_map/reduce_scatter | solution.py:40
  (132 shorter events, 36.2 us)
Async XLA Ops:
  7.2 17.6 %copy-start.28 = (bf16[6,128,256]{2,1,0:T(8,128)(2,1)S(1)}, bf16[6,128,256]{2,1,0:T(8,128)(2,1)}, u32[]{:S(2)}) copy-start(bf16[6,128,256]{2,1,0:T(8,128)(2,1)} %param.6) | copy-start | bytes 1179652
  7.2 227.8 %all-reduce.8.cloned.1.call-start = ((), (), s32[]{:S(2)}) async-start(), calls=%async_computation.13 | async-start | bytes 393216 | tf_op jit(solution)/shard_map/psum | solution.py:37
  24.8 33.1 %copy-start.22 = (bf16[1,512,512]{2,1,0:T(8,128)(2,1)}, bf16[1,512,512]{2,1,0:T(8,128)(2,1)S(1)}, u32[]{:S(2)}) copy-start(bf16[1,512,512]{2,1,0:T(8,128)(2,1)S(1)} %all-gather) | copy-start | bytes 1572868
  48.8 10.1 %copy-start.19 = (bf16[1,512,512]{2,1,0:T(8,128)(2,1)}, bf16[1,512,512]{2,1,0:T(8,128)(2,1)S(1)}, u32[]{:S(2)}) copy-start(bf16[1,512,512]{2,1,0:T(8,128)(2,1)S(1)} %all-gather.1) | copy-start | bytes 1572868
  48.8 9.8 %copy-start.25 = (bf16[6,256,512]{2,1,0:T(8,128)(2,1)S(1)}, bf16[6,256,512]{2,1,0:T(8,128)(2,1)}, u32[]{:S(2)}) copy-start(bf16[6,256,512]{2,1,0:T(8,128)(2,1)} %param.8) | copy-start | bytes 4718596
  48.8 9.8 %copy-start.26 = (bf16[6,32,256]{2,1,0:T(8,128)(2,1)S(1)}, bf16[6,32,256]{2,1,0:T(8,128)(2,1)}, u32[]{:S(2)}) copy-start(bf16[6,32,256]{2,1,0:T(8,128)(2,1)} %param.9) | copy-start | bytes 294916
  48.8 9.8 %copy-start.27 = (bf16[6,32,512]{2,1,0:T(8,128)(2,1)S(1)}, bf16[6,32,512]{2,1,0:T(8,128)(2,1)}, u32[]{:S(2)}) copy-start(bf16[6,32,512]{2,1,0:T(8,128)(2,1)} %param.10) | copy-start | bytes 589828
  58.6 15.5 %copy-start = (f32[256,512]{1,0:T(8,128)}, f32[256,512]{1,0:T(8,128)S(1)}, u32[]{:S(2)}) copy-start(f32[256,512]{1,0:T(8,128)S(1)} %fusion.18) | copy-start | bytes 1572868
  74.1 8.6 %copy-start.23 = (bf16[1,512,512]{2,1,0:T(8,128)(2,1)}, bf16[1,512,512]{2,1,0:T(8,128)(2,1)S(1)}, u32[]{:S(2)}) copy-start(bf16[1,512,512]{2,1,0:T(8,128)(2,1)S(1)} %all-gather.2) | copy-start | bytes 1572868
  82.4 24.6 %copy-start.3 = (f32[256,512]{1,0:T(8,128)}, f32[256,512]{1,0:T(8,128)S(1)}, u32[]{:S(2)}) copy-start(f32[256,512]{1,0:T(8,128)S(1)} %fusion.15) | copy-start | bytes 1572868
  97.7 8.9 %copy-start.20 = (bf16[1,512,512]{2,1,0:T(8,128)(2,1)}, bf16[1,512,512]{2,1,0:T(8,128)(2,1)S(1)}, u32[]{:S(2)}) copy-start(bf16[1,512,512]{2,1,0:T(8,128)(2,1)S(1)} %all-gather.3) | copy-start | bytes 1572868
  107.0 23.2 %copy-start.6 = (f32[256,512]{1,0:T(8,128)}, f32[256,512]{1,0:T(8,128)S(1)}, u32[]{:S(2)}) copy-start(f32[256,512]{1,0:T(8,128)S(1)} %fusion.12) | copy-start | bytes 1572868
  122.1 23.7 %copy-start.17 = (bf16[1,512,512]{2,1,0:T(8,128)(2,1)}, bf16[1,512,512]{2,1,0:T(8,128)(2,1)S(1)}, u32[]{:S(2)}) copy-start(bf16[1,512,512]{2,1,0:T(8,128)(2,1)S(1)} %all-gather.4) | copy-start | bytes 1572868
  130.5 24.4 %copy-start.9 = (f32[256,512]{1,0:T(8,128)}, f32[256,512]{1,0:T(8,128)S(1)}, u32[]{:S(2)}) copy-start(f32[256,512]{1,0:T(8,128)S(1)} %fusion.9) | copy-start | bytes 1572868
  145.8 10.6 %copy-start.15 = (bf16[1,512,512]{2,1,0:T(8,128)(2,1)}, bf16[1,512,512]{2,1,0:T(8,128)(2,1)S(1)}, u32[]{:S(2)}) copy-start(bf16[1,512,512]{2,1,0:T(8,128)(2,1)S(1)} %all-gather.5) | copy-start | bytes 1572868
  145.8 10.6 %copy-start.31 = (f32[6,512]{1,0:T(8,128)S(1)}, f32[6,512]{1,0:T(8,128)}, u32[]{:S(2)}) copy-start(f32[6,512]{1,0:T(8,128)} %param.11) | copy-start | bytes 36868
  184.1 5.1 %copy-start.4 = (f32[256,512]{1,0:T(8,128)S(1)}, f32[256,512]{1,0:T(8,128)}, u32[]{:S(2)}) copy-start(f32[256,512]{1,0:T(8,128)} %copy-done.3) | copy-start | bytes 1572868
  184.9 5.4 %copy-start.7 = (f32[256,512]{1,0:T(8,128)S(1)}, f32[256,512]{1,0:T(8,128)}, u32[]{:S(2)}) copy-start(f32[256,512]{1,0:T(8,128)} %copy-done.6) | copy-start | bytes 1572868
  187.0 4.3 copy-start.10
  193.4 105.4 %all-reduce.6.cloned.1.call-start = ((), (), s32[]{:S(2)}) async-start(), calls=%async_computation.12 | async-start | bytes 1572864 | tf_op jit(solution)/shard_map/psum | solution.py:25
  193.7 5.7 %copy-start.5 = (f32[256,512]{1,0:T(8,128)S(1)}, f32[256,512]{1,0:T(8,128)}, u32[]{:S(2)}) copy-start(f32[256,512]{1,0:T(8,128)} %copy-done.3) | copy-start | bytes 1572868
  196.6 4.6 copy-start.8
  198.4 4.7 copy-start.11
  200.3 4.6 copy-start.14
  205.9 119.8 %reduce-scatter.7.cloned.1.call-start = ((), (), s32[]{:S(2)}) async-start(), calls=%async_computation.6 | async-start | bytes 655360 | tf_op jit(solution)/shard_map/reduce_scatter | solution.py:40
  208.2 145.4 %reduce-scatter.9.cloned.1.call-start = ((), (), s32[]{:S(2)}) async-start(), calls=%async_computation.7 | async-start | bytes 655360 | tf_op jit(solution)/shard_map/reduce_scatter | solution.py:40
  210.5 170.9 %reduce-scatter.11.cloned.1.call-start = ((), (), s32[]{:S(2)}) async-start(), calls=%async_computation.8 | async-start | bytes 655360 | tf_op jit(solution)/shard_map/reduce_scatter | solution.py:40
  211.7 197.4 %reduce-scatter.13.cloned.1.call-start = ((), (), s32[]{:S(2)}) async-start(), calls=%async_computation.9 | async-start | bytes 655360 | tf_op jit(solution)/shard_map/reduce_scatter | solution.py:40
  213.0 224.2 %reduce-scatter.15.cloned.1.call-start = ((), (), s32[]{:S(2)}) async-start(), calls=%async_computation.10 | async-start | bytes 655360 | tf_op jit(solution)/shard_map/reduce_scatter | solution.py:40
  214.2 250.9 %reduce-scatter.17.cloned.1.call-start = ((), (), s32[]{:S(2)}) async-start(), calls=%async_computation.11 | async-start | bytes 655360 | tf_op jit(solution)/shard_map/reduce_scatter | solution.py:40
  239.5 226.5 %copy-start.32 = (f32[6,32,256]{2,1,0:T(8,128)}, f32[6,32,256]{2,1,0:T(8,128)S(1)}, u32[]{:S(2)}) copy-start(f32[6,32,256]{2,1,0:T(8,128)S(1)} %constant_dynamic-update-slice_fusion) | copy-start | bytes 589828
  304.1 161.9 %copy-start.29 = (f32[6,32,512]{2,1,0:T(8,128)}, f32[6,32,512]{2,1,0:T(8,128)S(1)}, u32[]{:S(2)}) copy-start(f32[6,32,512]{2,1,0:T(8,128)S(1)} %bitcast_dynamic-update-slice_fusion) | copy-start | bytes 1179652
  (9 other events, 15.9 us)
Sparse Core Ops, SparseCore 0:
  193.5 41.3 all-reduce.7
  238.9 59.8 all-reduce.5
  301.6 24.0 reduce-scatter.6
  328.4 25.1 reduce-scatter.8
  356.2 25.0 reduce-scatter.10
  384.0 25.1 reduce-scatter.12
  412.0 25.0 reduce-scatter.14
  439.9 25.0 reduce-scatter.16
where the time goes:
time: 475 us; the launch traced here: 474 us
  waiting for transfers between devices  235 us (49%)
  blocking collectives  171 us (36%)
  matrix products  33.3 us (7%)
  between operations  14.5 us (3%)
  other arithmetic  11.6 us (2%)
  local copies, waits for them, and re-layouts  7.98 us (2%)
    reduce_scatter x6, waiting for transfers between devices, one_layer(): lax.psum_scatter(lax.dot_general(scaled, weight_low, (((1,), (1,)), ((),...  156 us
    all_gather x6, blocking collectives, one_layer(): grads_all = lax.all_gather(grads, 'row', axis=0, tiled=True)  91.1 us
    psum x1, waiting for transfers between devices, one_layer(): lax.psum((squares_part, dots_part, inner_outer, inner_merged), 'row')  59.2 us
    all_gather x6, blocking collectives, one_layer(): lax.all_gather(acts, 'col', axis=0, tiled=True)  52.2 us
    psum x1, blocking collectives, one_layer(): lax.psum((squares_part, dots_part, inner_outer, inner_merged), 'row')  27.6 us
    psum x1, waiting for transfers between devices, one_layer(): in_grad = lax.psum(in_part, 'col')  18.9 us
  transfers between devices with their start and end apart: 8, of which 8 were waited for; matrix products, arithmetic and copies ran while one was open for 8% of the time, Pallas kernels for 0%

commit v1 on v0

--- a/solution.py
+++ b/solution.py
@@ -11,7 +11,13 @@
         adapt_in, adapt_out, (((0,), (0,)), ((), ())), preferred_element_type=jnp.float32
     )
     squares_part = jnp.sum(merged * merged, axis=0)
-    grads_all = lax.all_gather(grads, "row", axis=0, tiled=True)
+    size = lax.axis_size("row")
+    current, blocks = (grads, [grads])
+    for _ in range(size - 1):
+        current = lax.ppermute(current, "row", [(i, (i + 1) % size) for i in range(size)])
+        blocks.insert(0, current)
+    row_of_blocks = jnp.concatenate(blocks, axis=0)
+    grads_all = jnp.roll(row_of_blocks, (lax.axis_index("row") + 1) * grads.shape[0], axis=0)
     outer = lax.dot_general(
         lax.all_gather(acts, "col", axis=0, tiled=True),
         grads_all,

time: 475 us -> 440 us (0.926)
  blocking collectives: 171 us -> 80.3 us
  waiting for transfers between devices: 235 us -> 272 us
  starting transfers between devices: 0.51 us -> 13.1 us
    all_gather x6 -> x0, blocking collectives: 91.1 us -> none  [one_layer(): grads_all = lax.all_gather(grads, 'row', axis=0, tiled=True)]
    ppermute x0 -> x42, waiting for transfers between devices: none -> 28.3 us  [one_layer(): lax.ppermute(current, 'row', [(i, (i + 1) % size) for i in range(size)])]
    ppermute x0 -> x42, starting transfers between devices: none -> 12.8 us  [one_layer(): lax.ppermute(current, 'row', [(i, (i + 1) % size) for i in range(size)])]
    psum x1, waiting for transfers between devices: 18.9 us -> 28.1 us  [one_layer(): in_grad = lax.psum(in_part, 'col')]
  transfers between devices with their start and end apart: 8 -> 50, of which waited for: 8 -> 35; matrix products, arithmetic and copies ran while one was open for 8% -> 7% of each run, Pallas kernels for 0% -> 0%
where the time goes in v1:
time: 440 us; the launch traced here: 439 us
  waiting for transfers between devices  272 us (62%)
  blocking collectives  80.3 us (18%)
  matrix products  36.9 us (8%)
  between operations  14.9 us (3%)
  starting transfers between devices  13.1 us (3%)
  other arithmetic  11.6 us (3%)
  local copies, waits for them, and re-layouts  9.79 us (2%)
    reduce_scatter x6, waiting for transfers between devices, one_layer(): lax.psum_scatter(lax.dot_general(scaled, weight_low, (((1,), (1,)), ((),...  156 us
    psum x1, waiting for transfers between devices, one_layer(): lax.psum((squares_part, dots_part, inner_outer, inner_merged), 'row')  59.2 us
    all_gather x6, blocking collectives, one_layer(): lax.all_gather(acts, 'col', axis=0, tiled=True)  53.7 us
    ppermute x42, waiting for transfers between devices, one_layer(): lax.ppermute(current, 'row', [(i, (i + 1) % size) for i in range(size)])  28.3 us
    psum x1, waiting for transfers between devices, one_layer(): in_grad = lax.psum(in_part, 'col')  28.1 us
    psum x1, blocking collectives, one_layer(): lax.psum((squares_part, dots_part, inner_outer, inner_merged), 'row')  26.6 us
    ppermute x42, starting transfers between devices, one_layer(): lax.ppermute(current, 'row', [(i, (i + 1) % size) for i in range(size)])  12.8 us
    dot_general x6, matrix products, one_layer(): lax.dot_general(scaled, weight_low, (((1,), (1,)), ((), ())), preferred_e...  10.3 us
  transfers between devices with their start and end apart: 50, of which 35 were waited for; matrix products, arithmetic and copies ran while one was open for 7% of the time, Pallas kernels for 0%

profile of v1, /device:TPU:0, one launch (start us, length us, event | category | flops | bytes accessed | tf_op | source)
XLA Modules:
  0.0 438.8 jit_solution(14766243170486789337)
XLA Ops:
  8.8 2.7 collective-permute-start.28
  11.5 1.6 collective-permute-start.14
  13.2 1.5 collective-permute-done.35
  15.5 1.5 collective-permute-done.21
  18.7 1.6 collective-permute-done
  21.0 1.5 collective-permute-done.29
  24.1 1.6 collective-permute-done.8
  29.6 1.6 collective-permute-done.16
  35.1 1.6 collective-permute-done.24
  37.4 9.5 %all-gather = bf16[1,512,256]{2,1,0:T(8,128)(2,1)S(1)} all-gather(bf16[1,128,256]{2,1,0:T(8,128)(2,1)S(1)} %get-tuple-element.63), channel_id=2, replica_groups=mesh['row'=8,'col'=4] {'col'}, dimensions={1}, use_global_device_ids=true | all-gather | bytes 327680 | tf_op jit(solution)/shard_map/all_gather | solution.py:22
  46.9 9.0 %all-gather.1 = bf16[1,512,256]{2,1,0:T(8,128)(2,1)S(1)} all-gather(bf16[1,128,256]{2,1,0:T(8,128)(2,1)S(1)} %get-tuple-element.62), channel_id=3, replica_groups=mesh['row'=8,'col'=4] {'col'}, dimensions={1}, use_global_device_ids=true | all-gather | bytes 327680 | tf_op jit(solution)/shard_map/all_gather | solution.py:22
  56.5 1.7 collective-permute-start.40
  58.4 7.7 %all-gather.2 = bf16[1,512,256]{2,1,0:T(8,128)(2,1)S(1)} all-gather(bf16[1,128,256]{2,1,0:T(8,128)(2,1)S(1)} %get-tuple-element.61), channel_id=4, replica_groups=mesh['row'=8,'col'=4] {'col'}, dimensions={1}, use_global_device_ids=true | all-gather | bytes 327680 | tf_op jit(solution)/shard_map/all_gather | solution.py:22
  66.0 9.3 %all-gather.3 = bf16[1,512,256]{2,1,0:T(8,128)(2,1)S(1)} all-gather(bf16[1,128,256]{2,1,0:T(8,128)(2,1)S(1)} %get-tuple-element.60), channel_id=5, replica_groups=mesh['row'=8,'col'=4] {'col'}, dimensions={1}, use_global_device_ids=true | all-gather | bytes 327680 | tf_op jit(solution)/shard_map/all_gather | solution.py:22
  75.4 2.9 collective-permute-start.19
  78.6 9.4 %all-gather.4 = bf16[1,512,256]{2,1,0:T(8,128)(2,1)} all-gather(bf16[1,128,256]{2,1,0:T(8,128)(2,1)S(1)} %get-tuple-element.64), channel_id=6, replica_groups=mesh['row'=8,'col'=4] {'col'}, dimensions={1}, use_global_device_ids=true | all-gather | bytes 327680 | tf_op jit(solution)/shard_map/all_gather | solution.py:22
  87.9 9.0 %all-gather.5 = bf16[1,512,256]{2,1,0:T(8,128)(2,1)S(1)} all-gather(bf16[1,128,256]{2,1,0:T(8,128)(2,1)S(1)} %get-tuple-element.59), channel_id=7, replica_groups=mesh['row'=8,'col'=4] {'col'}, dimensions={1}, use_global_device_ids=true | all-gather | bytes 327680 | tf_op jit(solution)/shard_map/all_gather | solution.py:22
  99.1 3.4 collective-permute-done.34
  122.6 26.6 %all-reduce = (f32[512]{0:T(512)}, f32[512]{0:T(512)}, f32[512]{0:T(512)S(1)}, f32[512]{0:T(512)S(1)}, f32[512]{0:T(512)S(1)}, /*index=5*/f32[512]{0:T(512)S(1)}...) all-reduce(f32[512]{0:T(512)S(1)} %get-tuple-element.16, ...), channel_id=1, replica_groups=mesh['row'=8,'col'=4] {'row'}, use_global_device_ids=true, to_apply=%region_1.3 | all-reduce | flops 6144 | bytes 49152 | tf_op jit(solution)/shard_map/psum | solution.py:31
  150.0 2.2 convolution_bitcast_fusion.17
  152.2 2.1 convolution_bitcast_fusion.16
  158.7 2.0 convolution_bitcast_fusion.1
  160.7 2.3 fusion
  163.1 2.3 fusion.1
  172.1 28.1 %all-reduce.8.cloned.1.call-done = (f32[1,32,256]{2,1,0:T(8,128)}, f32[1,32,256]{2,1,0:T(8,128)}, f32[1,32,256]{2,1,0:T(8,128)}, f32[1,32,256]{2,1,0:T(8,128)}, ...) async-done(((f32[1,32,256]{2,1,0:T(8,128)}, f32[1,32,256]{2,1,0:T(8,128)}, f32[1,32,256]{2,1,0:T(8,128)}, f32[1,32,256]{2,1,0:T(8,128)}, f32[1,32,256]{2,1,0:T(8,128)}, ...) | async-done | bytes 196624 | tf_op jit(solution)/shard_map/psum | solution.py:43
  204.7 59.2 %all-reduce.6.cloned.1.call-done = (f32[32,512]{1,0:T(8,128)}, f32[32,512]{1,0:T(8,128)}, f32[32,512]{1,0:T(8,128)}, f32[32,512]{1,0:T(8,128)}, f32[32,512]{1,0:...) async-done(((f32[32,512]{1,0:T(8,128)}, f32[32,512]{1,0:T(8,128)}, ...) | async-done | bytes 786448 | tf_op jit(solution)/shard_map/psum | solution.py:31
  269.3 21.6 %reduce-scatter.7.cloned.1.call-done = f32[128,256]{1,0:T(8,128)} async-done(((f32[512,256]{1,0:T(8,128)}), f32[128,256]{1,0:T(8,128)}) %reduce-scatter.7.cloned.1.call-update) | async-done | bytes 131088 | tf_op jit(solution)/shard_map/reduce_scatter | solution.py:46
  291.9 26.9 %reduce-scatter.9.cloned.1.call-done = f32[128,256]{1,0:T(8,128)} async-done(((f32[512,256]{1,0:T(8,128)}), f32[128,256]{1,0:T(8,128)}) %reduce-scatter.9.cloned.1.call-update) | async-done | bytes 131088 | tf_op jit(solution)/shard_map/reduce_scatter | solution.py:46
  319.7 26.9 %reduce-scatter.11.cloned.1.call-done = f32[128,256]{1,0:T(8,128)} async-done(((f32[512,256]{1,0:T(8,128)}), f32[128,256]{1,0:T(8,128)}) %reduce-scatter.11.cloned.1.call-update) | async-done | bytes 131088 | tf_op jit(solution)/shard_map/reduce_scatter | solution.py:46
  347.5 26.9 %reduce-scatter.13.cloned.1.call-done = f32[128,256]{1,0:T(8,128)} async-done(((f32[512,256]{1,0:T(8,128)}), f32[128,256]{1,0:T(8,128)}) %reduce-scatter.13.cloned.1.call-update) | async-done | bytes 131088 | tf_op jit(solution)/shard_map/reduce_scatter | solution.py:46
  375.3 27.0 %reduce-scatter.15.cloned.1.call-done = f32[128,256]{1,0:T(8,128)} async-done(((f32[512,256]{1,0:T(8,128)}), f32[128,256]{1,0:T(8,128)}) %reduce-scatter.15.cloned.1.call-update) | async-done | bytes 131088 | tf_op jit(solution)/shard_map/reduce_scatter | solution.py:46
  403.2 27.0 %reduce-scatter.17.cloned.1.call-done = f32[128,256]{1,0:T(8,128)} async-done(((f32[512,256]{1,0:T(8,128)}), f32[128,256]{1,0:T(8,128)}) %reduce-scatter.17.cloned.1.call-update) | async-done | bytes 131088 | tf_op jit(solution)/shard_map/reduce_scatter | solution.py:46
  (249 shorter events, 65.6 us)
Async XLA Ops:
  7.2 193.0 %all-reduce.8.cloned.1.call-start = ((), (), s32[]{:S(2)}) async-start(), calls=%async_computation.13 | async-start | bytes 393216 | tf_op jit(solution)/shard_map/psum | solution.py:43
  8.3 6.5 %collective-permute-start.35 = (bf16[64,512]{1,0:T(8,128)(2,1)S(1)}, bf16[64,512]{1,0:T(8,128)(2,1)S(1)}, u32[]{:S(2)}, u32[]{:S(2)}) collective-permute-start(bf16[64,512]{1,0:T(8,128)(2,1)S(1)} %get-tuple-element.53), channel_id=1, source_target_pairs={{0,4},{4,8},{8,12},{12,16},{16,20},{20,24},{24,28},{28,0},{1,5},{5... | collective-permute-start | bytes 196616 | tf_op jit(solution)/shard_map/ppermute | solution.py:17
  8.8 6.7 %collective-permute-start.28 = (bf16[64,512]{1,0:T(8,128)(2,1)S(1)}, bf16[64,512]{1,0:T(8,128)(2,1)S(1)}, u32[]{:S(2)}, u32[]{:S(2)}) collective-permute-start(bf16[64,512]{1,0:T(8,128)(2,1)S(1)} %get-tuple-element.58), channel_id=1, source_target_pairs={{0,4},{4,8},{8,12},{12,16},{16,20},{20,24},{24,28},{28,0},{1,5},{5... | collective-permute-start | bytes 196616 | tf_op jit(solution)/shard_map/ppermute | solution.py:17
  11.5 6.1 %collective-permute-start.14 = (bf16[64,512]{1,0:T(8,128)(2,1)S(1)}, bf16[64,512]{1,0:T(8,128)(2,1)S(1)}, u32[]{:S(2)}, u32[]{:S(2)}) collective-permute-start(bf16[64,512]{1,0:T(8,128)(2,1)S(1)} %get-tuple-element.55), channel_id=1, source_target_pairs={{0,4},{4,8},{8,12},{12,16},{16,20},{20,24},{24,28},{28,0},{1,5},{5... | collective-permute-start | bytes 196616 | tf_op jit(solution)/shard_map/ppermute | solution.py:17
  15.5 5.5 %collective-permute-start.36 = (bf16[64,512]{1,0:T(8,128)(2,1)S(1)}, bf16[64,512]{1,0:T(8,128)(2,1)S(1)}, u32[]{:S(2)}, u32[]{:S(2)}) collective-permute-start(bf16[64,512]{1,0:T(8,128)(2,1)S(1)} %collective-permute-done.35), channel_id=1, source_target_pairs={{0,4},{4,8},{8,12},{12,16},{16,20},{20,24},{24,28},{28,0},{1,5},{5... | collective-permute-start | bytes 196616 | tf_op jit(solution)/shard_map/ppermute | solution.py:17
  33.4 22.4 %collective-permute-start.10 = (bf16[64,512]{1,0:T(8,128)(2,1)S(1)}, bf16[64,512]{1,0:T(8,128)(2,1)S(1)}, u32[]{:S(2)}, u32[]{:S(2)}) collective-permute-start(bf16[64,512]{1,0:T(8,128)(2,1)S(1)} %collective-permute-done.9), channel_id=1, source_target_pairs={{0,4},{4,8},{8,12},{12,16},{16,20},{20,24},{24,28},{28,0},{1,5},{5... | collective-permute-start | bytes 196616 | tf_op jit(solution)/shard_map/ppermute | solution.py:17
  34.1 21.8 %collective-permute-start.3 = (bf16[64,512]{1,0:T(8,128)(2,1)S(1)}, bf16[64,512]{1,0:T(8,128)(2,1)S(1)}, u32[]{:S(2)}, u32[]{:S(2)}) collective-permute-start(bf16[64,512]{1,0:T(8,128)(2,1)S(1)} %collective-permute-done.2), channel_id=1, source_target_pairs={{0,4},{4,8},{8,12},{12,16},{16,20},{20,24},{24,28},{28,0},{1,5},{5... | collective-permute-start | bytes 196616 | tf_op jit(solution)/shard_map/ppermute | solution.py:17
  35.1 21.3 %collective-permute-start.39 = (bf16[64,512]{1,0:T(8,128)(2,1)S(1)}, bf16[64,512]{1,0:T(8,128)(2,1)S(1)}, u32[]{:S(2)}, u32[]{:S(2)}) collective-permute-start(bf16[64,512]{1,0:T(8,128)(2,1)S(1)} %collective-permute-done.38), channel_id=1, source_target_pairs={{0,4},{4,8},{8,12},{12,16},{16,20},{20,24},{24,28},{28,0},{1,5},{5... | collective-permute-start | bytes 196616 | tf_op jit(solution)/shard_map/ppermute | solution.py:17
  36.7 19.8 %collective-permute-start.32 = (bf16[64,512]{1,0:T(8,128)(2,1)S(1)}, bf16[64,512]{1,0:T(8,128)(2,1)S(1)}, u32[]{:S(2)}, u32[]{:S(2)}) collective-permute-start(bf16[64,512]{1,0:T(8,128)(2,1)S(1)} %collective-permute-done.31), channel_id=1, source_target_pairs={{0,4},{4,8},{8,12},{12,16},{16,20},{20,24},{24,28},{28,0},{1,5},{5... | collective-permute-start | bytes 196616 | tf_op jit(solution)/shard_map/ppermute | solution.py:17
  37.4 20.9 %collective-permute-start.25 = (bf16[64,512]{1,0:T(8,128)(2,1)S(1)}, bf16[64,512]{1,0:T(8,128)(2,1)S(1)}, u32[]{:S(2)}, u32[]{:S(2)}) collective-permute-start(bf16[64,512]{1,0:T(8,128)(2,1)S(1)} %collective-permute-done.24), channel_id=1, source_target_pairs={{0,4},{4,8},{8,12},{12,16},{16,20},{20,24},{24,28},{28,0},{1,5},{5... | collective-permute-start | bytes 196616 | tf_op jit(solution)/shard_map/ppermute | solution.py:17
  55.9 19.4 %collective-permute-start.18 = (bf16[64,512]{1,0:T(8,128)(2,1)S(1)}, bf16[64,512]{1,0:T(8,128)(2,1)S(1)}, u32[]{:S(2)}, u32[]{:S(2)}) collective-permute-start(bf16[64,512]{1,0:T(8,128)(2,1)S(1)} %collective-permute-done.17), channel_id=1, source_target_pairs={{0,4},{4,8},{8,12},{12,16},{16,20},{20,24},{24,28},{28,0},{1,5},{5... | collective-permute-start | bytes 196616 | tf_op jit(solution)/shard_map/ppermute | solution.py:17
  55.9 19.4 %collective-permute-start.11 = (bf16[64,512]{1,0:T(8,128)(2,1)S(1)}, bf16[64,512]{1,0:T(8,128)(2,1)S(1)}, u32[]{:S(2)}, u32[]{:S(2)}) collective-permute-start(bf16[64,512]{1,0:T(8,128)(2,1)S(1)} %collective-permute-done.10), channel_id=1, source_target_pairs={{0,4},{4,8},{8,12},{12,16},{16,20},{20,24},{24,28},{28,0},{1,5},{5... | collective-permute-start | bytes 196616 | tf_op jit(solution)/shard_map/ppermute | solution.py:17
  56.5 21.9 %collective-permute-start.4 = (bf16[64,512]{1,0:T(8,128)(2,1)S(1)}, bf16[64,512]{1,0:T(8,128)(2,1)S(1)}, u32[]{:S(2)}, u32[]{:S(2)}) collective-permute-start(bf16[64,512]{1,0:T(8,128)(2,1)S(1)} %collective-permute-done.3), channel_id=1, source_target_pairs={{0,4},{4,8},{8,12},{12,16},{16,20},{20,24},{24,28},{28,0},{1,5},{5... | collective-permute-start | bytes 196616 | tf_op jit(solution)/shard_map/ppermute | solution.py:17
  56.5 21.9 %collective-permute-start.40 = (bf16[64,512]{1,0:T(8,128)(2,1)S(1)}, bf16[64,512]{1,0:T(8,128)(2,1)S(1)}, u32[]{:S(2)}, u32[]{:S(2)}) collective-permute-start(bf16[64,512]{1,0:T(8,128)(2,1)S(1)} %collective-permute-done.39), channel_id=1, source_target_pairs={{0,4},{4,8},{8,12},{12,16},{16,20},{20,24},{24,28},{28,0},{1,5},{5... | collective-permute-start | bytes 196616 | tf_op jit(solution)/shard_map/ppermute | solution.py:17
  58.3 20.2 %collective-permute-start.33 = (bf16[64,512]{1,0:T(8,128)(2,1)S(1)}, bf16[64,512]{1,0:T(8,128)(2,1)S(1)}, u32[]{:S(2)}, u32[]{:S(2)}) collective-permute-start(bf16[64,512]{1,0:T(8,128)(2,1)S(1)} %collective-permute-done.32), channel_id=1, source_target_pairs={{0,4},{4,8},{8,12},{12,16},{16,20},{20,24},{24,28},{28,0},{1,5},{5... | collective-permute-start | bytes 196616 | tf_op jit(solution)/shard_map/ppermute | solution.py:17
  75.3 21.6 %collective-permute-start.26 = (bf16[64,512]{1,0:T(8,128)(2,1)S(1)}, bf16[64,512]{1,0:T(8,128)(2,1)S(1)}, u32[]{:S(2)}, u32[]{:S(2)}) collective-permute-start(bf16[64,512]{1,0:T(8,128)(2,1)S(1)} %collective-permute-done.25), channel_id=1, source_target_pairs={{0,4},{4,8},{8,12},{12,16},{16,20},{20,24},{24,28},{28,0},{1,5},{5... | collective-permute-start | bytes 196616 | tf_op jit(solution)/shard_map/ppermute | solution.py:17
  75.4 21.6 %collective-permute-start.19 = (bf16[64,512]{1,0:T(8,128)(2,1)S(1)}, bf16[64,512]{1,0:T(8,128)(2,1)S(1)}, u32[]{:S(2)}, u32[]{:S(2)}) collective-permute-start(bf16[64,512]{1,0:T(8,128)(2,1)S(1)} %collective-permute-done.18), channel_id=1, source_target_pairs={{0,4},{4,8},{8,12},{12,16},{16,20},{20,24},{24,28},{28,0},{1,5},{5... | collective-permute-start | bytes 196616 | tf_op jit(solution)/shard_map/ppermute | solution.py:17
  78.3 19.3 %collective-permute-start.12 = (bf16[64,512]{1,0:T(8,128)(2,1)S(1)}, bf16[64,512]{1,0:T(8,128)(2,1)S(1)}, u32[]{:S(2)}, u32[]{:S(2)}) collective-permute-start(bf16[64,512]{1,0:T(8,128)(2,1)S(1)} %collective-permute-done.11), channel_id=1, source_target_pairs={{0,4},{4,8},{8,12},{12,16},{16,20},{20,24},{24,28},{28,0},{1,5},{5... | collective-permute-start | bytes 196616 | tf_op jit(solution)/shard_map/ppermute | solution.py:17
  78.4 19.3 %collective-permute-start.5 = (bf16[64,512]{1,0:T(8,128)(2,1)S(1)}, bf16[64,512]{1,0:T(8,128)(2,1)S(1)}, u32[]{:S(2)}, u32[]{:S(2)}) collective-permute-start(bf16[64,512]{1,0:T(8,128)(2,1)S(1)} %collective-permute-done.4), channel_id=1, source_target_pairs={{0,4},{4,8},{8,12},{12,16},{16,20},{20,24},{24,28},{28,0},{1,5},{5... | collective-permute-start | bytes 196616 | tf_op jit(solution)/shard_map/ppermute | solution.py:17
  78.5 20.2 %collective-permute-start.41 = (bf16[64,512]{1,0:T(8,128)(2,1)S(1)}, bf16[64,512]{1,0:T(8,128)(2,1)S(1)}, u32[]{:S(2)}, u32[]{:S(2)}) collective-permute-start(bf16[64,512]{1,0:T(8,128)(2,1)S(1)} %collective-permute-done.40), channel_id=1, source_target_pairs={{0,4},{4,8},{8,12},{12,16},{16,20},{20,24},{24,28},{28,0},{1,5},{5... | collective-permute-start | bytes 196616 | tf_op jit(solution)/shard_map/ppermute | solution.py:17
  96.9 5.5 %collective-permute-start.34 = (bf16[64,512]{1,0:T(8,128)(2,1)S(1)}, bf16[64,512]{1,0:T(8,128)(2,1)S(1)}, u32[]{:S(2)}, u32[]{:S(2)}) collective-permute-start(bf16[64,512]{1,0:T(8,128)(2,1)S(1)} %collective-permute-done.33), channel_id=1, source_target_pairs={{0,4},{4,8},{8,12},{12,16},{16,20},{20,24},{24,28},{28,0},{1,5},{5... | collective-permute-start | bytes 196616 | tf_op jit(solution)/shard_map/ppermute | solution.py:17
  97.0 6.2 %collective-permute-start.27 = (bf16[64,512]{1,0:T(8,128)(2,1)S(1)}, bf16[64,512]{1,0:T(8,128)(2,1)S(1)}, u32[]{:S(2)}, u32[]{:S(2)}) collective-permute-start(bf16[64,512]{1,0:T(8,128)(2,1)S(1)} %collective-permute-done.26), channel_id=1, source_target_pairs={{0,4},{4,8},{8,12},{12,16},{16,20},{20,24},{24,28},{28,0},{1,5},{5... | collective-permute-start | bytes 196616 | tf_op jit(solution)/shard_map/ppermute | solution.py:17
  97.6 6.2 %collective-permute-start.20 = (bf16[64,512]{1,0:T(8,128)(2,1)S(1)}, bf16[64,512]{1,0:T(8,128)(2,1)S(1)}, u32[]{:S(2)}, u32[]{:S(2)}) collective-permute-start(bf16[64,512]{1,0:T(8,128)(2,1)S(1)} %collective-permute-done.19), channel_id=1, source_target_pairs={{0,4},{4,8},{8,12},{12,16},{16,20},{20,24},{24,28},{28,0},{1,5},{5... | collective-permute-start | bytes 196616 | tf_op jit(solution)/shard_map/ppermute | solution.py:17
  97.7 6.9 %collective-permute-start.13 = (bf16[64,512]{1,0:T(8,128)(2,1)S(1)}, bf16[64,512]{1,0:T(8,128)(2,1)S(1)}, u32[]{:S(2)}, u32[]{:S(2)}) collective-permute-start(bf16[64,512]{1,0:T(8,128)(2,1)S(1)} %collective-permute-done.12), channel_id=1, source_target_pairs={{0,4},{4,8},{8,12},{12,16},{16,20},{20,24},{24,28},{28,0},{1,5},{5... | collective-permute-start | bytes 196616 | tf_op jit(solution)/shard_map/ppermute | solution.py:17
  98.7 6.5 %collective-permute-start.6 = (bf16[64,512]{1,0:T(8,128)(2,1)S(1)}, bf16[64,512]{1,0:T(8,128)(2,1)S(1)}, u32[]{:S(2)}, u32[]{:S(2)}) collective-permute-start(bf16[64,512]{1,0:T(8,128)(2,1)S(1)} %collective-permute-done.5), channel_id=1, source_target_pairs={{0,4},{4,8},{8,12},{12,16},{16,20},{20,24},{24,28},{28,0},{1,5},{5... | collective-permute-start | bytes 196616 | tf_op jit(solution)/shard_map/ppermute | solution.py:17
  158.6 105.4 %all-reduce.6.cloned.1.call-start = ((), (), s32[]{:S(2)}) async-start(), calls=%async_computation.12 | async-start | bytes 1572864 | tf_op jit(solution)/shard_map/psum | solution.py:31
  160.7 130.3 %reduce-scatter.7.cloned.1.call-start = ((), (), s32[]{:S(2)}) async-start(), calls=%async_computation.6 | async-start | bytes 655360 | tf_op jit(solution)/shard_map/reduce_scatter | solution.py:46
  163.1 155.7 %reduce-scatter.9.cloned.1.call-start = ((), (), s32[]{:S(2)}) async-start(), calls=%async_computation.7 | async-start | bytes 655360 | tf_op jit(solution)/shard_map/reduce_scatter | solution.py:46
  165.5 181.1 %reduce-scatter.11.cloned.1.call-start = ((), (), s32[]{:S(2)}) async-start(), calls=%async_computation.8 | async-start | bytes 655360 | tf_op jit(solution)/shard_map/reduce_scatter | solution.py:46
  167.0 207.4 %reduce-scatter.13.cloned.1.call-start = ((), (), s32[]{:S(2)}) async-start(), calls=%async_computation.9 | async-start | bytes 655360 | tf_op jit(solution)/shard_map/reduce_scatter | solution.py:46
  168.5 233.9 %reduce-scatter.15.cloned.1.call-start = ((), (), s32[]{:S(2)}) async-start(), calls=%async_computation.10 | async-start | bytes 655360 | tf_op jit(solution)/shard_map/reduce_scatter | solution.py:46
  170.0 260.3 %reduce-scatter.17.cloned.1.call-start = ((), (), s32[]{:S(2)}) async-start(), calls=%async_computation.11 | async-start | bytes 655360 | tf_op jit(solution)/shard_map/reduce_scatter | solution.py:46
  (49 other events, 659.4 us)
Sparse Core Ops, SparseCore 0:
  158.7 41.3 all-reduce.7
  204.1 59.8 all-reduce.5
  266.8 24.0 reduce-scatter.6
  293.6 25.1 reduce-scatter.8
  321.4 25.0 reduce-scatter.10
  349.2 25.1 reduce-scatter.12
  377.2 25.0 reduce-scatter.14
  405.2 25.0 reduce-scatter.16
